TPU v7x, 32 devices: a whole 2x2x4 slice. The times are simulated.
32 devices in a mesh: dp: 8 (over z, x), expert: 4 (over y, core).
Axes of the slice: x: 2, y: 2, z: 4, core: 2. Of those that a mesh axis runs over, the one named last changes fastest.
Arguments:
- tokens: bfloat16 [2048, 2048], P('dp'), may hold values from -6 to 6
- routes: int32 [2048, 6], P('dp'), may hold values from 0 to 63, all different within a row; in each aligned block of 256 rows (0 to 255, 256 to 511, ...) at most 32 rows name the same one
- gates: float32 [2048, 6], P('dp'), may hold values from 0.1 to 1
- w_gate: bfloat16 [64, 2048, 1408], P('dp', None, 'expert'), may hold values from -0.125 to 0.125
- w_up: bfloat16 [64, 2048, 1408], P('dp', None, 'expert'), may hold values from -0.125 to 0.125
- w_down: bfloat16 [64, 1408, 2048], P('dp', 'expert'), may hold values from -0.21875 to 0.21875
- s_gate: bfloat16 [2048, 2816], P(None, 'expert'), may hold values from -0.125 to 0.125
- s_up: bfloat16 [2048, 2816], P(None, 'expert'), may hold values from -0.125 to 0.125
- s_down: bfloat16 [2816, 2048], P('expert'), may hold values from -0.15625 to 0.15625
Outputs:
- mixed: bfloat16 [2048, 2048], P('dp', 'expert')
Inputs may be any that keep to these rules, and one draw needn't show every extreme that they name: `routes`: each row names 6 different experts. Within each aligned block of 256 rows (the rows of one index of dp) no expert is named by more than 32 rows; some expert is named by exactly 32 rows in some block of every draw.
All inputs are finite; a program needn't handle non-finite values.
Results may differ from a plain program's by a relative error of at most 0.013.
Values may be sent and summed in bfloat16 or wider, within the bound.
A program may use at most 128 MiB of HBM per device.

v0:
```python
import jax
import jax.numpy as jnp
from jax import lax
from jax.sharding import PartitionSpec as P

CAP = 32


def body(tokens, routes, gates, w_gate, w_up, w_down, s_gate, s_up, s_down):
    tok_rows, width = tokens.shape
    local_experts = w_gate.shape[0]
    groups = lax.axis_size("dp")
    members = lax.axis_size("expert")
    experts_all = local_experts * groups
    top_count = routes.shape[1]
    capacity = CAP
    quarter = width // members
    labels = jnp.arange(experts_all, dtype=jnp.int32)
    matches = (routes[:, :, None] == labels[None, None, :]).astype(jnp.int32)
    counts = jnp.sum(matches, axis=1)
    before = jnp.cumsum(counts, axis=0) - counts
    slots = jnp.sum(matches * before[:, None, :], axis=2)
    dest = routes * capacity + slots
    token_ids = jnp.repeat(jnp.arange(tok_rows, dtype=jnp.int32), top_count)
    sources = (
        jnp.full((experts_all * capacity,), tok_rows, jnp.int32).at[dest.reshape(-1)].set(token_ids)
    )
    padded = jnp.concatenate([tokens, jnp.zeros((1, width), tokens.dtype)], axis=0)
    outgoing = padded[sources].reshape(groups, local_experts, capacity, width)
    offset = lax.axis_index("expert") * quarter
    outgoing = lax.dynamic_slice_in_dim(outgoing, offset, quarter, 3)
    received = lax.all_to_all(outgoing, "dp", split_axis=0, concat_axis=0, tiled=True)
    received = lax.all_gather(received, "expert", axis=3, tiled=True)
    gate = jnp.einsum("sjcd,jdf->sjcf", received, w_gate, preferred_element_type=jnp.float32)
    up = jnp.einsum("sjcd,jdf->sjcf", received, w_up, preferred_element_type=jnp.float32)
    hidden = (jax.nn.silu(gate) * up).astype(jnp.bfloat16)
    partial_value = jnp.einsum("sjcf,jfd->sjcd", hidden, w_down, preferred_element_type=jnp.float32)
    summed = lax.psum_scatter(
        partial_value.astype(jnp.bfloat16), "expert", scatter_dimension=3, tiled=True
    )
    returned = lax.all_to_all(summed, "dp", split_axis=0, concat_axis=0, tiled=True)
    flat = returned.reshape(experts_all * capacity, quarter)
    picked = flat[dest].astype(jnp.float32)
    routed = jnp.einsum("tk,tkd->td", gates, picked)
    shared_gate = jnp.dot(tokens, s_gate, preferred_element_type=jnp.float32)
    shared_up = jnp.dot(tokens, s_up, preferred_element_type=jnp.float32)
    shared_hidden = (jax.nn.silu(shared_gate) * shared_up).astype(jnp.bfloat16)
    shared_part = jnp.dot(shared_hidden, s_down, preferred_element_type=jnp.float32)
    shared_out = lax.psum_scatter(
        shared_part.astype(jnp.bfloat16), "expert", scatter_dimension=1, tiled=True
    ).astype(jnp.float32)
    return (shared_out + routed).astype(jnp.bfloat16)


def solution(mesh):
    placed = (
        P("dp", None),
        P("dp", None),
        P("dp", None),
        P("dp", None, "expert"),
        P("dp", None, "expert"),
        P("dp", "expert", None),
        P(None, "expert"),
        P(None, "expert"),
        P("expert", None),
    )
    return jax.shard_map(
        body, mesh=mesh, in_specs=placed, out_specs=P("dp", "expert"), check_vma=False
    )
```

profile of v0, /device:TPU:0, one launch (start us, length us, event | category | flops | bytes accessed | tf_op | source)
XLA Modules:
  0.0 341.5 jit_solution(1969258154155409684)
XLA Ops:
  6.5 0.9 convert_reduce_fusion
  7.5 0.6 reduce-window.6
  8.4 0.8 select_reduce_fusion
  9.1 0.7 compare_select_fusion.1
  10.3 6.2 %scatter_custom_fusion = s32[2048]{0:T(1024)S(1)} fusion(s32[1536]{0:T(1024)S(1)} %fusion.19, s32[1536]{0:T(1024)S(1)} %reshape.78, s32[]{:T(128)} %constant.11.clone.1), kind=kCustom, calls=%fused_computation.38 | custom fusion | bytes 8196 | tf_op jit(solution)/shard_map/scatter | solution.py:26
  16.5 2.4 concatenate.3
  19.0 17.7 %gather_fusion = bf16[2048,2048]{1,0:T(8,128)(2,1)} fusion(bf16[257,2048]{1,0:T(8,128)(2,1)} %concatenate.3, s32[2048]{0:T(1024)S(1)} %fusion.18), kind=kCustom, calls=%fused_computation | custom fusion | bytes 16785408 | tf_op jit(solution)/shard_map/gather | solution.py:29
  36.7 1.8 constant_dynamic-slice_fusion
  38.5 55.3 %all_to_all.10 = bf16[8,8,32,512]{3,2,1,0:T(8,128)(2,1)S(1)} all-to-all(bf16[8,8,32,512]{3,2,1,0:T(8,128)(2,1)S(1)} %constant_dynamic-slice_fusion), channel_id=1, replica_groups=mesh['dp'=8,'expert'=4] {'dp'}, dimensions={0} | all-to-all | bytes 4194304 | tf_op jit(solution)/shard_map/all_to_all | solution.py:32
  93.8 1.6 copy.30
  95.7 57.2 %all-gather.2.cloned.1.call-done = bf16[8,8,32,2048]{3,2,0,1:T(8,128)(2,1)} async-done(((bf16[8,8,32,512]{3,2,0,1:T(8,128)(2,1)}), bf16[8,8,32,2048]{3,2,0,1:T(8,128)(2,1)}) %all-gather.2.cloned.1.call-update) | async-done | bytes 8388624 | tf_op jit(solution)/shard_map/all_gather | solution.py:33
  152.9 12.9 %fusion.4 = f32[8,8,32,352]{3,2,1,0:T(8,128)} fusion(bf16[8,8,32,2048]{3,2,0,1:T(8,128)(2,1)} %all-gather.2.cloned.1.call-done, bf16[8,2048,352]{1,2,0:T(8,128)(2,1)} %param.12), kind=kOutput, calls=%fused_computation.7 | convolution fusion | flops 2952790016 | bytes 22806528 | tf_op jit(solution)/shard_map/sjcd,jdf->sjcf/dot_general | solution.py:34
  165.9 13.3 %fusion.8 = bf16[8,8,32,352]{3,2,0,1:T(8,128)(2,1)} fusion(f32[8,8,32,352]{3,2,1,0:T(8,128)} %fusion.4, bf16[8,8,32,2048]{3,2,0,1:T(8,128)(2,1)} %all-gather.2.cloned.1.call-done, bf16[8,2048,352]{1,2,0:T(8,128)(2,1)} %param.13), kind=kOutput, calls=%fused_computation.11 | convolution fusion | flops 2957115392 | bytes 24248320 | tf_op jit(solution)/shard_map/sjcd,jdf->sjcf/dot_general | solution.py:35
  179.1 12.5 %convert_bitcast_fusion = bf16[8,8,32,2048]{3,2,0,1:T(8,128)(2,1)} fusion(bf16[8,8,32,352]{3,2,0,1:T(8,128)(2,1)} %fusion.8, bf16[8,352,2048]{2,1,0:T(8,128)(2,1)} %param.14), kind=kOutput, calls=%fused_computation.9 | convolution fusion | flops 2956984320 | bytes 21364736 | tf_op jit(solution)/shard_map/sjcf,jfd->sjcd/dot_general | solution.py:37
  191.7 71.4 %reduce-scatter.5.cloned.1.call-done = bf16[8,8,32,512]{3,2,0,1:T(8,128)(2,1)} async-done(((bf16[8,8,32,2048]{3,2,0,1:T(8,128)(2,1)}), bf16[8,8,32,512]{3,2,0,1:T(8,128)(2,1)}) %reduce-scatter.5.cloned.1.call-update) | async-done | bytes 2097168 | tf_op jit(solution)/shard_map/reduce_scatter | solution.py:38
  263.0 3.1 copy.31
  266.2 5.5 %all-to-all-start.1 = ((bf16[8,8,32,512]{3,2,1,0:T(8,128)(2,1)}), bf16[8,8,32,512]{3,2,1,0:T(8,128)(2,1)}, u32[]{:S(2)}, u32[]{:S(2)}) async-start(bf16[8,8,32,512]{3,2,1,0:T(8,128)(2,1)} %copy.31), calls=%async_computation.3 | async-start | bytes 4194304 | tf_op jit(solution)/shard_map/all_to_all | solution.py:41
  272.0 4.0 %fusion.23 = f32[256,704]{0,1:T(8,128)} fusion(bf16[256,2048]{1,0:T(8,128)(2,1)} %param.9, bf16[2048,704]{0,1:T(8,128)(2,1)} %param.15), kind=kOutput, calls=%fused_computation.42 | convolution fusion | flops 738197504 | bytes 4653056 | tf_op jit(solution)/shard_map/dot_general | solution.py:45
  275.9 6.6 %convolution_convert_fusion = bf16[256,2048]{1,0:T(8,128)(2,1)} fusion(bf16[704,2048]{1,0:T(8,128)(2,1)S(1)} %copy-done, bf16[256,2048]{1,0:T(8,128)(2,1)} %param.9, bf16[2048,704]{0,1:T(8,128)(2,1)} %param.16, f32[256,704]{0,1:T(8,128)} %fusion.23), kind=kOutput, calls=%fused_computation.17 | convolution fusion | flops 1478000640 | bytes 8585216 | tf_op jit(solution)/shard_map/dot_general | solution.py:48
  283.0 36.9 %all-to-all-done.1 = bf16[8,8,32,512]{3,2,1,0:T(8,128)(2,1)} async-done(((bf16[8,8,32,512]{3,2,1,0:T(8,128)(2,1)}), bf16[8,8,32,512]{3,2,1,0:T(8,128)(2,1)}, u32[]{:S(2)}, u32[]{:S(2)}) %all-to-all-start.1) | async-done | bytes 2097184 | tf_op jit(solution)/shard_map/all_to_all | solution.py:41
  319.9 7.4 %gather_fusion.1 = bf16[1536,512]{1,0:T(8,128)(2,1)} fusion(bf16[2048,512]{1,0:T(8,128)(2,1)} %bitcast.12, s32[2048]{0:T(1024)S(1)} %pad_clamp_fusion), kind=kCustom, calls=%fused_computation.1 | custom fusion | bytes 3151872 | tf_op jit(solution)/shard_map/gather | solution.py:43
  327.2 3.7 %reshape.67 = bf16[256,6,512]{2,1,0:T(8,128)(2,1)} reshape(bf16[1536,512]{1,0:T(8,128)(2,1)} %gather_fusion.1) | data formatting | bytes 3145728 | tf_op jit(solution)/shard_map/gather | solution.py:43
  331.0 2.3 fusion.24
  333.3 1.7 fusion.15
  (26 shorter events, 1.8 us)
Async XLA Ops:
  6.5 269.4 %copy-start = (bf16[704,2048]{1,0:T(8,128)(2,1)S(1)}, bf16[704,2048]{1,0:T(8,128)(2,1)}, u32[]{:S(2)}) copy-start(bf16[704,2048]{1,0:T(8,128)(2,1)} %param.17) | copy-start | bytes 8650756
  6.5 146.4 %all-gather.2.cloned.1.call-start = ((), (), s32[]{:S(2)}) async-start(), calls=%async_computation.5 | async-start | bytes 10485760 | tf_op jit(solution)/shard_map/all_gather | solution.py:33
  95.5 167.6 %reduce-scatter.5.cloned.1.call-start = ((), (), s32[]{:S(2)}) async-start(), calls=%async_computation.6 | async-start | bytes 10485760 | tf_op jit(solution)/shard_map/reduce_scatter | solution.py:38
  266.2 53.7 %all-to-all-start.1 = ((bf16[8,8,32,512]{3,2,1,0:T(8,128)(2,1)}), bf16[8,8,32,512]{3,2,1,0:T(8,128)(2,1)}, u32[]{:S(2)}, u32[]{:S(2)}) async-start(bf16[8,8,32,512]{3,2,1,0:T(8,128)(2,1)} %copy.31), calls=%async_computation.3 | async-start | bytes 4194304 | tf_op jit(solution)/shard_map/all_to_all | solution.py:41
  271.7 61.6 %reduce-scatter.3.cloned.1.call-start = ((), (), s32[]{:S(2)}) async-start(), calls=%async_computation.4 | async-start | bytes 1310720 | tf_op jit(solution)/shard_map/reduce_scatter | solution.py:49
  275.9 6.9 %copy-start.1 = (f32[256,6]{0,1:T(8,128)S(1)}, f32[256,6]{0,1:T(8,128)}, u32[]{:S(2)}) copy-start(f32[256,6]{0,1:T(8,128)} %param.11) | copy-start | bytes 18436
Sparse Core Ops, SparseCore 0:
  95.6 57.2 all-gather.1
  191.8 71.2 reduce-scatter.4
  282.7 25.0 reduce-scatter.2
where the time goes:
time: 342 us
  waiting for transfers between devices  166 us (49%)
  blocking collectives  55.3 us (16%)
  matrix products  51.5 us (15%)
  local copies, waits for them, and re-layouts  45.1 us (13%)
  between operations  13.3 us (4%)
  starting transfers between devices  5.99 us (2%)
  other arithmetic  4.86 us (1%)
    reduce_scatter x1, waiting for transfers between devices, body(): lax.psum_scatter(partial_value.astype(jnp.bfloat16), 'expert', scatter_di...  71.4 us
    all_gather x1, waiting for transfers between devices, body(): received = lax.all_gather(received, 'expert', axis=3, tiled=True)  57.2 us
    all_to_all x1, blocking collectives, body(): lax.all_to_all(outgoing, 'dp', split_axis=0, concat_axis=0, tiled=True)  55.3 us
    all_to_all x1, waiting for transfers between devices, body(): lax.all_to_all(summed, 'dp', split_axis=0, concat_axis=0, tiled=True)  36.9 us
    gather x1, local copies, waits for them, and re-layouts, body(): outgoing = padded[sources].reshape(groups, local_experts, capacity, width)  17.7 us
    dot_general x1, matrix products, body(): jnp.einsum('sjcd,jdf->sjcf', received, w_up, preferred_element_type=jnp.f...  13.3 us
    dot_general x1, matrix products, body(): jnp.einsum('sjcd,jdf->sjcf', received, w_gate, preferred_element_type=jnp...  12.9 us
    dot_general x1, matrix products, body(): jnp.einsum('sjcf,jfd->sjcd', hidden, w_down, preferred_element_type=jnp.f...  12.5 us
  transfers between devices with their start and end apart: 4, of which 3 were waited for; matrix products, arithmetic and copies ran while one was open for 7% of the time, Pallas kernels for 0%

commit v1 on v0

--- a/solution.py
+++ b/solution.py
@@ -30,7 +30,8 @@
     offset = lax.axis_index("expert") * quarter
     outgoing = lax.dynamic_slice_in_dim(outgoing, offset, quarter, 3)
     received = lax.all_to_all(outgoing, "dp", split_axis=0, concat_axis=0, tiled=True)
-    received = lax.all_gather(received, "expert", axis=3, tiled=True)
+    parts = lax.all_gather(received, "expert", axis=0, tiled=False)
+    received = jnp.concatenate(parts, axis=3)
     gate = jnp.einsum("sjcd,jdf->sjcf", received, w_gate, preferred_element_type=jnp.float32)
     up = jnp.einsum("sjcd,jdf->sjcf", received, w_up, preferred_element_type=jnp.float32)
     hidden = (jax.nn.silu(gate) * up).astype(jnp.bfloat16)

time: 342 us -> 366 us (1.070)
  local copies, waits for them, and re-layouts: 45.1 us -> 68.8 us
    reshape x1 -> x3, local copies, waits for them, and re-layouts: 0.01 us -> 25.4 us  [the longest x2 25.4 us: body(): received = jnp.concatenate(parts, axis=3)]
where the time goes in v1:
time: 366 us; the launch traced here: 365 us
  waiting for transfers between devices  166 us (45%)
  local copies, waits for them, and re-layouts  68.8 us (19%)
  blocking collectives  55.4 us (15%)
  matrix products  51.5 us (14%)
  between operations  13.3 us (4%)
  starting transfers between devices  5.81 us (2%)
  other arithmetic  4.86 us (1%)
    reduce_scatter x1, waiting for transfers between devices, body(): lax.psum_scatter(partial_value.astype(jnp.bfloat16), 'expert', scatter_di...  71.4 us
    all_gather x1, waiting for transfers between devices, body(): parts = lax.all_gather(received, 'expert', axis=0, tiled=False)  57.4 us
    all_to_all x1, blocking collectives, body(): lax.all_to_all(outgoing, 'dp', split_axis=0, concat_axis=0, tiled=True)  55.4 us
    all_to_all x1, waiting for transfers between devices, body(): lax.all_to_all(summed, 'dp', split_axis=0, concat_axis=0, tiled=True)  36.9 us
    reshape x2, local copies, waits for them, and re-layouts, body(): received = jnp.concatenate(parts, axis=3)  25.4 us
    gather x1, local copies, waits for them, and re-layouts, body(): outgoing = padded[sources].reshape(groups, local_experts, capacity, width)  17.7 us
    dot_general x1, matrix products, body(): jnp.einsum('sjcd,jdf->sjcf', received, w_up, preferred_element_type=jnp.f...  13.3 us
    dot_general x1, matrix products, body(): jnp.einsum('sjcd,jdf->sjcf', received, w_gate, preferred_element_type=jnp...  12.9 us
  transfers between devices with their start and end apart: 4, of which 3 were waited for; matrix products, arithmetic and copies ran while one was open for 7% of the time, Pallas kernels for 0%

profile of v1, /device:TPU:0, one launch (start us, length us, event | category | flops | bytes accessed | tf_op | source)
XLA Modules:
  0.0 365.4 jit_solution(10229589518241858550)
XLA Ops:
  6.5 0.9 convert_reduce_fusion
  8.4 0.8 select_reduce_fusion
  9.1 0.7 compare_select_fusion.1
  10.3 6.2 %scatter_custom_fusion = s32[2048]{0:T(1024)S(1)} fusion(s32[1536]{0:T(1024)S(1)} %fusion.19, s32[1536]{0:T(1024)S(1)} %reshape.86, s32[]{:T(128)} %constant.11.clone.1), kind=kCustom, calls=%fused_computation.38 | custom fusion | bytes 8196 | tf_op jit(solution)/shard_map/scatter | solution.py:26
  16.5 2.4 concatenate.3
  19.0 17.7 %gather_fusion = bf16[2048,2048]{1,0:T(8,128)(2,1)} fusion(bf16[257,2048]{1,0:T(8,128)(2,1)} %concatenate.3, s32[2048]{0:T(1024)S(1)} %fusion.18), kind=kCustom, calls=%fused_computation | custom fusion | bytes 16785408 | tf_op jit(solution)/shard_map/gather | solution.py:29
  36.7 1.8 constant_dynamic-slice_fusion
  38.5 55.4 %all_to_all.10 = bf16[8,8,32,512]{3,2,1,0:T(8,128)(2,1)} all-to-all(bf16[8,8,32,512]{3,2,1,0:T(8,128)(2,1)S(1)} %constant_dynamic-slice_fusion), channel_id=1, replica_groups=mesh['dp'=8,'expert'=4] {'dp'}, dimensions={0} | all-to-all | bytes 4194304 | tf_op jit(solution)/shard_map/all_to_all | solution.py:32
  94.0 57.4 %all-gather.3.cloned.1.call-done = bf16[32,8,32,512]{3,2,1,0:T(8,128)(2,1)} async-done(((bf16[8,8,32,512]{3,2,1,0:T(8,128)(2,1)}), bf16[32,8,32,512]{3,2,1,0:T(8,128)(2,1)}) %all-gather.3.cloned.1.call-update) | async-done | bytes 8388624 | tf_op jit(solution)/shard_map/all_gather | solution.py:33
  151.4 11.1 %copy.30 = bf16[8,8,32,4,512]{4,3,2,0,1:T(4,128)(2,1)} copy(bf16[8,8,32,4,512]{4,2,1,0,3:T(8,128)(2,1)} %bitcast.78) | data formatting | bytes 16777216 | tf_op jit(solution)/shard_map/reshape | solution.py:34
  162.5 14.3 %reshape.64 = bf16[8,8,32,2048]{3,2,0,1:T(8,128)(2,1)} reshape(bf16[8,8,32,4,512]{4,3,2,0,1:T(4,128)(2,1)} %copy.30) | data formatting | bytes 16777216 | tf_op jit(solution)/shard_map/reshape | solution.py:34
  176.8 12.9 %fusion.4 = f32[8,8,32,352]{3,2,1,0:T(8,128)} fusion(bf16[8,8,32,2048]{3,2,0,1:T(8,128)(2,1)} %reshape.64, bf16[8,2048,352]{1,2,0:T(8,128)(2,1)} %param.12), kind=kOutput, calls=%fused_computation.7 | convolution fusion | flops 2952790016 | bytes 22806528 | tf_op jit(solution)/shard_map/sjcd,jdf->sjcf/dot_general | solution.py:35
  189.7 13.3 %fusion.8 = bf16[8,8,32,352]{3,2,0,1:T(8,128)(2,1)} fusion(f32[8,8,32,352]{3,2,1,0:T(8,128)} %fusion.4, bf16[8,8,32,2048]{3,2,0,1:T(8,128)(2,1)} %reshape.64, bf16[8,2048,352]{1,2,0:T(8,128)(2,1)} %param.13), kind=kOutput, calls=%fused_computation.11 | convolution fusion | flops 2957115392 | bytes 24248320 | tf_op jit(solution)/shard_map/sjcd,jdf->sjcf/dot_general | solution.py:36
  203.0 12.5 %convert_bitcast_fusion = bf16[8,8,32,2048]{3,2,0,1:T(8,128)(2,1)} fusion(bf16[8,8,32,352]{3,2,0,1:T(8,128)(2,1)} %fusion.8, bf16[8,352,2048]{2,1,0:T(8,128)(2,1)} %param.14), kind=kOutput, calls=%fused_computation.9 | convolution fusion | flops 2956984320 | bytes 21364736 | tf_op jit(solution)/shard_map/sjcf,jfd->sjcd/dot_general | solution.py:38
  215.6 71.4 %reduce-scatter.5.cloned.1.call-done = bf16[8,8,32,512]{3,2,0,1:T(8,128)(2,1)} async-done(((bf16[8,8,32,2048]{3,2,0,1:T(8,128)(2,1)}), bf16[8,8,32,512]{3,2,0,1:T(8,128)(2,1)}) %reduce-scatter.5.cloned.1.call-update) | async-done | bytes 2097168 | tf_op jit(solution)/shard_map/reduce_scatter | solution.py:39
  286.9 3.1 copy.31
  290.1 5.5 %all-to-all-start.1 = ((bf16[8,8,32,512]{3,2,1,0:T(8,128)(2,1)}), bf16[8,8,32,512]{3,2,1,0:T(8,128)(2,1)}, u32[]{:S(2)}, u32[]{:S(2)}) async-start(bf16[8,8,32,512]{3,2,1,0:T(8,128)(2,1)} %copy.31), calls=%async_computation.3 | async-start | bytes 4194304 | tf_op jit(solution)/shard_map/all_to_all | solution.py:42
  295.8 4.0 %fusion.23 = f32[256,704]{0,1:T(8,128)} fusion(bf16[256,2048]{1,0:T(8,128)(2,1)} %param.9, bf16[2048,704]{0,1:T(8,128)(2,1)} %param.15), kind=kOutput, calls=%fused_computation.42 | convolution fusion | flops 738197504 | bytes 4653056 | tf_op jit(solution)/shard_map/dot_general | solution.py:46
  299.8 6.6 %convolution_convert_fusion = bf16[256,2048]{1,0:T(8,128)(2,1)} fusion(bf16[704,2048]{1,0:T(8,128)(2,1)S(1)} %copy-done, bf16[256,2048]{1,0:T(8,128)(2,1)} %param.9, bf16[2048,704]{0,1:T(8,128)(2,1)} %param.16, f32[256,704]{0,1:T(8,128)} %fusion.23), kind=kOutput, calls=%fused_computation.17 | convolution fusion | flops 1478000640 | bytes 8585216 | tf_op jit(solution)/shard_map/dot_general | solution.py:49
  306.9 36.9 %all-to-all-done.1 = bf16[8,8,32,512]{3,2,1,0:T(8,128)(2,1)} async-done(((bf16[8,8,32,512]{3,2,1,0:T(8,128)(2,1)}), bf16[8,8,32,512]{3,2,1,0:T(8,128)(2,1)}, u32[]{:S(2)}, u32[]{:S(2)}) %all-to-all-start.1) | async-done | bytes 2097184 | tf_op jit(solution)/shard_map/all_to_all | solution.py:42
  343.8 7.4 %gather_fusion.1 = bf16[1536,512]{1,0:T(8,128)(2,1)} fusion(bf16[2048,512]{1,0:T(8,128)(2,1)} %bitcast.14, s32[2048]{0:T(1024)S(1)} %pad_clamp_fusion), kind=kCustom, calls=%fused_computation.1 | custom fusion | bytes 3151872 | tf_op jit(solution)/shard_map/gather | solution.py:44
  351.1 3.7 %reshape.75 = bf16[256,6,512]{2,1,0:T(8,128)(2,1)} reshape(bf16[1536,512]{1,0:T(8,128)(2,1)} %gather_fusion.1) | data formatting | bytes 3145728 | tf_op jit(solution)/shard_map/gather | solution.py:44
  354.9 2.3 fusion.24
  357.2 1.7 fusion.15
  (27 shorter events, 2.2 us)
Async XLA Ops:
  6.5 293.3 %copy-start = (bf16[704,2048]{1,0:T(8,128)(2,1)S(1)}, bf16[704,2048]{1,0:T(8,128)(2,1)}, u32[]{:S(2)}) copy-start(bf16[704,2048]{1,0:T(8,128)(2,1)} %param.17) | copy-start | bytes 8650756
  6.5 144.9 %all-gather.3.cloned.1.call-start = ((), (), s32[]{:S(2)}) async-start(), calls=%async_computation.6 | async-start | bytes 10485760 | tf_op jit(solution)/shard_map/all_gather | solution.py:33
  94.0 193.0 %reduce-scatter.5.cloned.1.call-start = ((), (), s32[]{:S(2)}) async-start(), calls=%async_computation.5 | async-start | bytes 10485760 | tf_op jit(solution)/shard_map/reduce_scatter | solution.py:39
  290.1 53.7 %all-to-all-start.1 = ((bf16[8,8,32,512]{3,2,1,0:T(8,128)(2,1)}), bf16[8,8,32,512]{3,2,1,0:T(8,128)(2,1)}, u32[]{:S(2)}, u32[]{:S(2)}) async-start(bf16[8,8,32,512]{3,2,1,0:T(8,128)(2,1)} %copy.31), calls=%async_computation.3 | async-start | bytes 4194304 | tf_op jit(solution)/shard_map/all_to_all | solution.py:42
  295.6 61.6 %reduce-scatter.3.cloned.1.call-start = ((), (), s32[]{:S(2)}) async-start(), calls=%async_computation.4 | async-start | bytes 1310720 | tf_op jit(solution)/shard_map/reduce_scatter | solution.py:50
  299.8 6.9 %copy-start.1 = (f32[256,6]{0,1:T(8,128)S(1)}, f32[256,6]{0,1:T(8,128)}, u32[]{:S(2)}) copy-start(f32[256,6]{0,1:T(8,128)} %param.11) | copy-start | bytes 18436
Sparse Core Ops, SparseCore 0:
  94.1 57.2 all-gather.2
  215.7 71.2 reduce-scatter.4
  306.6 25.0 reduce-scatter.2
